TPU v7x, 512 devices: a whole 4x4x16 slice. The times are simulated.
512 devices in a mesh: ctx: 64 (over z, y_hi, core), req: 8 (over y_lo, x).
Axes of the slice: x: 4, y: 4 (y_hi: 2, y_lo: 2; y = y_hi * 2 + y_lo), z: 16, core: 2. Of those that a mesh axis runs over, the one named last changes fastest.
Arguments:
- hidden: bfloat16 [1024, 5120], P('req'), parts along dimension 0, may hold values from -6 to 6
- w_query: bfloat16 [5120, 8192], P(None, 'ctx'), may hold values from -0.078125 to 0.078125
- key_projection_weight: bfloat16 [5120, 1024], P(None, 'ctx'), may hold values from -0.078125 to 0.078125
- value_projection_weight: bfloat16 [5120, 1024], P(None, 'ctx'), may hold values from -0.078125 to 0.078125
- query_gain: float32 [128], replicated, may hold values from 0.5 to 1.5
- key_gain: float32 [128], replicated, may hold values from 4 to 8
- stored_cache_keys: bfloat16 [65536, 1024], P(('req', 'ctx')), parts along dimension 0, may hold values from -100 to 100
- stored_cache_values: bfloat16 [65536, 1024], P(('req', 'ctx')), parts along dimension 0, may hold values from -8 to 8
- cache_length: int32 [8], P('req'), parts along dimension 0, may hold values from 4096 to 8192
- first_position: int32 [8], P('req'), parts along dimension 0, may hold values from 0 to 4095
Outputs:
- attended: bfloat16 [1024, 8192], P('req', 'ctx'), parts along dimension 0
There are 8 independent parts, one for each index of `req`. A program takes and returns all parts, laid end to end along the dimension named above; an argument that names none is the same for every part. Nothing has to cross between parts.
All inputs are finite; a program needn't handle non-finite values.
Results may differ from a plain program's by a relative error of at most 0.013.
The roundings to bfloat16 on the way count: a program that leaves them out, or rounds other values in their place, can miss the bound.
Values may be sent and summed in bfloat16 or wider, within the bound.
No kernel may reach another device: no remote copies, remote signals or barrier semaphores. Data moves between devices by JAX's collectives and lax.ppermute only.
A program may use at most 128 MiB of HBM per device.

v0:
```python
import math
import jax
import jax.numpy as jnp
from jax import lax
from jax.sharding import Mesh
from jax.sharding import PartitionSpec as P

CTX = ("ctx_0", "ctx_1", "ctx_2")
REQ_CTX = ("req", "ctx_0", "ctx_1", "ctx_2")


def gather_turned(arrays, axis, dims):
    turned = [jnp.moveaxis(a, dim, 0) for a, dim in zip(arrays, dims)]
    widths = [t[0].size for t in turned]
    both = jnp.concatenate([t.reshape(-1, w) for t, w in zip(turned, widths)], axis=1)
    filled = lax.all_gather(both, axis, axis=0, tiled=True)
    pieces = jnp.split(filled, [sum(widths[:k]) for k in range(1, len(widths))], axis=1)
    return tuple(
        (
            jnp.moveaxis(b.reshape(-1, *t.shape[1:]), 0, dim)
            for b, t, dim in zip(pieces, turned, dims)
        )
    )


def laid_out(pieces, dim):
    shape = list(pieces.shape[1:])
    shape[dim] *= pieces.shape[0]
    return jnp.moveaxis(pieces, 0, dim).reshape(shape)


def gather_in_order(value, axes, turns):
    pieces = value
    for k in turns:
        pieces = lax.all_gather(pieces, axes[k])
    done = turns[::-1]
    back = [done.index(k) for k in range(len(axes))]
    pieces = pieces.transpose(*back, *range(len(axes), pieces.ndim))
    return pieces.reshape(-1, *value.shape)


def gather_axes(value, axes, turns, dim):
    return laid_out(gather_in_order(value, axes, turns), dim)


def sent_together(arrays, axis, split_dim, concat_dim, along):
    columns = [a.reshape(*a.shape[:along], -1) for a in arrays]
    both = jnp.concatenate(columns, axis=along)
    filled, at, outs = (
        lax.all_to_all(both, axis, split_axis=split_dim, concat_axis=concat_dim, tiled=True),
        0,
        [],
    )
    for a, column in zip(arrays, columns):
        section = filled[..., at : at + column.shape[along]]
        outs.append(section.reshape(*section.shape[:along], *a.shape[along:]))
        at += column.shape[along]
    return tuple(outs)


def normalize(joined_values, gain):
    mean_square = jnp.mean(joined_values * joined_values, axis=-1, keepdims=True)
    return joined_values * lax.rsqrt(mean_square + 1e-06) * gain


def rotate(joined_values, positions):
    half = joined_values.shape[-1] // 2
    freq = jnp.exp(
        jnp.arange(half, dtype=jnp.float32) * (-2.0 * math.log(1000000.0) / joined_values.shape[-1])
    )
    angles = positions[:, None] * freq[None, :]
    cosine = jnp.concatenate([jnp.cos(angles), jnp.cos(angles)], axis=-1)[:, None, :]
    sine = jnp.concatenate([jnp.sin(angles), jnp.sin(angles)], axis=-1)[:, None, :]
    turned = jnp.concatenate([-joined_values[..., half:], joined_values[..., :half]], axis=-1)
    return joined_values * cosine + turned * sine


def soft_weights(scores, visible):
    masked = jnp.where(visible, scores, -1e30)
    top = jnp.max(masked, axis=-1)
    weights = jnp.where(visible, jnp.exp(masked - top[..., None]), 0.0)
    return (weights, top, jnp.sum(weights, axis=-1))


def join(first, second):
    top = jnp.maximum(first[1], second[1])
    scale_a = jnp.exp(first[1] - top)
    scale_b = jnp.exp(second[1] - top)
    summed = first[0] * scale_a[..., None] + second[0] * scale_b[..., None]
    return (summed, top, first[2] * scale_a + second[2] * scale_b)


def fold_sources(received):
    sums, maxima, totals = received
    top = jnp.max(maxima, axis=1)
    factor = jnp.exp(maxima - top[:, None])
    return (jnp.sum(sums * factor[..., None], axis=1), top, jnp.sum(totals * factor, axis=1))


def per_device(
    hidden,
    w_query,
    key_projection_weight,
    value_projection_weight,
    query_gain,
    key_gain,
    stored_cache_keys,
    stored_cache_values,
    cache_length,
    first_position,
):
    groups = lax.axis_size(CTX)
    rank = lax.axis_index(CTX)
    input_tokens = hidden.shape[0]
    head_dim = query_gain.shape[0]
    heads_here = w_query.shape[1] // head_dim
    all_heads = heads_here * groups
    kv_heads = stored_cache_keys.shape[1] // head_dim
    query_group = all_heads // kv_heads
    slots = stored_cache_keys.shape[0]
    scale = 1.0 / math.sqrt(head_dim)
    positions = first_position[0].astype(jnp.float32) + jnp.arange(input_tokens, dtype=jnp.float32)
    projected = jnp.dot(hidden, w_query, preferred_element_type=jnp.float32).reshape(
        input_tokens, heads_here, head_dim
    )
    own_queries = (
        rotate(normalize(projected, query_gain), positions).astype(jnp.bfloat16).transpose(1, 0, 2)
    )
    key_part = jnp.dot(hidden, key_projection_weight, preferred_element_type=jnp.float32).astype(
        jnp.bfloat16
    )
    value_part = jnp.dot(
        hidden, value_projection_weight, preferred_element_type=jnp.float32
    ).astype(jnp.bfloat16)
    key_full, value_full = gather_turned((key_part, value_part), CTX, (1, 1))
    key_float = (
        key_full.astype(jnp.float32).reshape(input_tokens, head_dim, kv_heads).transpose(0, 2, 1)
    )
    incoming_keys = rotate(normalize(key_float, key_gain), positions).astype(jnp.bfloat16)
    incoming_values = value_full.reshape(input_tokens, head_dim, kv_heads).transpose(0, 2, 1)
    query_states = gather_axes(own_queries, CTX, (1, 0, 2), 0)
    token_rows = query_states.reshape(kv_heads, query_group * input_tokens, head_dim)
    valid = (rank * slots + jnp.arange(slots, dtype=jnp.int32) < cache_length[0])[None, :]

    def shard_term(index):
        query_rows = lax.dynamic_index_in_dim(token_rows, index, 0, keepdims=False)
        key_rows = lax.dynamic_slice_in_dim(stored_cache_keys, index * head_dim, head_dim, 1)
        value_rows = lax.dynamic_slice_in_dim(stored_cache_values, index * head_dim, head_dim, 1)
        scores = (
            lax.dot_general(
                query_rows, key_rows, (((1,), (1,)), ((), ())), preferred_element_type=jnp.float32
            )
            * scale
        )
        weights, top, total = soft_weights(scores, valid)
        summed = jnp.dot(
            weights.astype(jnp.bfloat16), value_rows, preferred_element_type=jnp.float32
        )
        return (summed, top, total)

    sums, maxima, totals = lax.map(shard_term, jnp.arange(kv_heads, dtype=jnp.int32))
    sums = sums.reshape(all_heads, input_tokens, head_dim)
    maxima = maxima.reshape(all_heads, input_tokens)
    totals = totals.reshape(all_heads, input_tokens)
    received = sent_together((sums[:, None], maxima[:, None], totals[:, None]), CTX, 0, 1, 3)
    merged = fold_sources(received)
    head_ids = rank * heads_here + jnp.arange(heads_here, dtype=jnp.int32)
    chosen = head_ids // query_group
    keys_here = jnp.take(incoming_keys, chosen, axis=1)
    values_here = jnp.take(incoming_values, chosen, axis=1)
    scores = (
        jnp.einsum("htd,shd->hts", own_queries, keys_here, preferred_element_type=jnp.float32)
        * scale
    )
    causal = (jnp.arange(input_tokens)[None, :] <= jnp.arange(input_tokens)[:, None])[None]
    weights, top, total = soft_weights(scores, causal)
    fresh = jnp.einsum(
        "hts,shd->htd",
        weights.astype(jnp.bfloat16),
        values_here,
        preferred_element_type=jnp.float32,
    )
    final = join((fresh, top, total), merged)
    attention_output = final[0] / final[2][..., None]
    return (
        attention_output.transpose(1, 0, 2)
        .reshape(input_tokens, heads_here * head_dim)
        .astype(jnp.bfloat16)
    )


def solution(mesh):
    finer = Mesh(
        mesh.devices.reshape(16, 2, 2, mesh.shape["req"]), ("ctx_0", "ctx_1", "ctx_2", "req")
    )
    return jax.shard_map(
        per_device,
        mesh=finer,
        in_specs=(
            P("req", None),
            P(None, CTX),
            P(None, CTX),
            P(None, CTX),
            P(),
            P(),
            P(REQ_CTX, None),
            P(REQ_CTX, None),
            P("req"),
            P("req"),
        ),
        out_specs=P("req", CTX),
        check_vma=False,
    )
```

profile of v0, /device:TPU:1, one launch (start us, length us, event | category | flops | bytes accessed | tf_op | source)
XLA Modules:
  0.0 499.5 jit_solution(5183464044391376757)
XLA Ops:
  6.5 1.3 copy-done
  7.9 2.0 multiply_reduce_fusion.1
  9.8 0.7 fusion.28
  11.4 1.3 pad_maximum_fusion.1
  12.7 5.7 %all-gather = bf16[256,128]{0,1:T(8,128)(2,1)S(1)} all-gather(bf16[128,128]{0,1:T(8,128)(2,1)S(1)} %get-tuple-element.125), channel_id=2, replica_groups=mesh['ctx_0'=16,'ctx_1'=2,'ctx_2'=2,'req'=8] {'ctx_1'}, dimensions={0}, use_global_device_ids=true | all-gather | bytes 98304 | tf_op jit(solution)/shard_map/all_gather | solution.py:35
  18.5 0.7 copy.70
  19.2 66.1 %all-gather.6.cloned.1.call-done = bf16[32,1,128,128]{3,2,1,0:T(8,128)(2,1)} async-done(((bf16[2,1,128,128]{3,2,1,0:T(8,128)(2,1)}), bf16[32,1,128,128]{3,2,1,0:T(8,128)(2,1)}) %all-gather.6.cloned.1.call-update) | async-done | bytes 1048592 | tf_op jit(solution)/shard_map/all_gather | solution.py:35
  85.4 31.9 %all-gather.8.cloned.1.call-done = bf16[32,2,1,128,128]{4,3,2,1,0:T(8,128)(2,1)} async-done(((bf16[16,2,1,128,128]{4,3,2,1,0:T(8,128)(2,1)}), bf16[32,2,1,128,128]{4,3,2,1,0:T(8,128)(2,1)}) %all-gather.8.cloned.1.call-update) | async-done | bytes 2097168 | tf_op jit(solution)/shard_map/all_gather | solution.py:35
  117.3 1.7 copy.64
  119.1 69.1 %while.16 = (s32[]{:T(128)}, f32[8,1024,128]{2,1,0:T(8,128)}, f32[8,1024]{1,0:T(8,128)S(1)}, f32[8,1024]{1,0:T(8,128)}, s32[8]{0:T(128)S(1)}, /*index=5*/bf16[8,...) while((s32[]{:T(128)}, f32[8,1024,128]{2,1,0:T(8,128)}, ...), condition=%wide.region_6.8_spmd.clone, body=%wide.region_3.7_spmd.clone.sunk | while | flops 68286728 | bytes 2459269 | solution.py:161
  119.1 0.7 dynamic_slice.37
  122.5 0.7 compare_bitcast_fusion.2
  123.2 1.0 fusion.75
  124.2 1.9 fusion.76
  126.2 1.4 dynamic_update_slice.20
  127.7 0.7 dynamic_slice.37
  131.2 0.7 compare_bitcast_fusion.2
  131.8 1.0 fusion.75
  132.8 2.0 fusion.76
  134.9 1.4 dynamic_update_slice.20
  136.4 0.7 dynamic_slice.37
  139.9 0.7 compare_bitcast_fusion.2
  140.5 1.0 fusion.75
  141.5 1.9 fusion.76
  143.6 1.4 dynamic_update_slice.20
  145.0 0.7 dynamic_slice.37
  148.5 0.7 compare_bitcast_fusion.2
  149.1 1.0 fusion.75
  150.2 1.9 fusion.76
  152.2 1.4 dynamic_update_slice.20
  153.7 0.7 dynamic_slice.37
  157.1 0.7 compare_bitcast_fusion.2
  157.7 1.0 fusion.75
  158.8 1.9 fusion.76
  160.8 1.4 dynamic_update_slice.20
  162.3 0.7 dynamic_slice.37
  165.7 0.7 compare_bitcast_fusion.2
  166.4 1.0 fusion.75
  167.4 1.9 fusion.76
  169.4 1.4 dynamic_update_slice.20
  170.9 0.7 dynamic_slice.37
  174.4 0.7 compare_bitcast_fusion.2
  175.0 1.0 fusion.75
  176.0 1.9 fusion.76
  178.1 1.4 dynamic_update_slice.20
  179.5 0.7 dynamic_slice.37
  183.0 0.7 compare_bitcast_fusion.2
  183.6 1.0 fusion.75
  184.7 1.9 fusion.76
  186.7 1.4 dynamic_update_slice.20
  188.2 6.0 %reshape_broadcast_in_dim_reshape.8 = f32[64,1,128,1]{3,2,0,1:T(8,128)} reshape(f32[8,1024]{1,0:T(8,128)S(1)} %get-tuple-element.56) | data formatting | bytes 65536 | tf_op jit(solution)/shard_map/reshape;broadcast_in_dim;reshape | solution.py:47
  194.2 6.1 %reshape_broadcast_in_dim_reshape.9 = f32[64,1,128,1]{3,2,0,1:T(8,128)} reshape(f32[8,1024]{1,0:T(8,128)S(1)} %copy-done.4) | data formatting | bytes 65536 | tf_op jit(solution)/shard_map/reshape;broadcast_in_dim;reshape | solution.py:47
  200.3 7.6 %pad_maximum_fusion = f32[64,1,128,130]{3,2,0,1:T(8,128)} fusion(f32[64,1,128,1]{3,2,0,1:T(8,128)} %reshape_broadcast_in_dim_reshape.9, f32[64,1,128,1]{3,2,0,1:T(8,128)} %reshape_broadcast_in_dim_reshape.8, f32[64,1,128,128]{3,2,0,1:T(8,128)} %bitcast.98), kind=kLoop, calls=%fused_computation.19 | loop fusion | flops 2129920 | bytes 8519680 | tf_op jit(solution)/shard_map/concatenate | solution.py:48
  207.9 12.4 %copy.67 = f32[64,1,128,130]{2,1,3,0:T(1,128)} copy(f32[64,1,128,130]{3,2,0,1:T(8,128)} %pad_maximum_fusion) | data formatting | bytes 8519680 | tf_op jit(solution)/shard_map/concatenate | solution.py:48
  220.2 14.7 %all-to-all-start = ((f32[64,1,128,130]{2,1,3,0:T(1,128)}), f32[64,1,128,130]{2,1,3,0:T(1,128)}, u32[]{:S(2)}, u32[]{:S(2)}) async-start(f32[64,1,128,130]{2,1,3,0:T(1,128)} %copy.67), calls=%async_computation | async-start | bytes 8519680 | tf_op jit(solution)/shard_map/all_to_all | solution.py:50
  235.2 0.4 convolution_convert_fusion
  235.7 0.5 convolution_convert_fusion.1
  236.1 250.6 %all_gather.18 = bf16[1024,256]{1,0:T(8,128)(2,1)S(1)} all-gather(bf16[16,256]{1,0:T(8,128)(2,1)S(1)} %pad_maximum_fusion.3), channel_id=1, replica_groups=mesh['ctx_0'=16,'ctx_1'=2,'ctx_2'=2,'req'=8] {'ctx_0','ctx_1','ctx_2'}, dimensions={0}, use_global_device_ids=true | all-gather | bytes 532480 | tf_op jit(solution)/shard_map/all_gather | solution.py:16
  486.8 0.2 copy.58
  487.0 0.2 copy.61
  487.9 0.2 fusion.60
  488.1 2.8 copy.72
  491.0 0.7 fusion.17
  491.9 0.8 fusion.21
  (55 shorter events, 2.8 us)
Async XLA Ops:
  6.5 1.3 copy-start
  6.5 78.8 %all-gather.6.cloned.1.call-start = ((), (), s32[]{:S(2)}) async-start(), calls=%async_computation.1 | async-start | bytes 1114112 | tf_op jit(solution)/shard_map/all_gather | solution.py:35
  19.2 98.1 %all-gather.8.cloned.1.call-start = ((), (), s32[]{:S(2)}) async-start(), calls=%async_computation.2 | async-start | bytes 3145728 | tf_op jit(solution)/shard_map/all_gather | solution.py:35
  188.2 6.1 %copy-start.4 = (f32[8,1024]{1,0:T(8,128)S(1)}, f32[8,1024]{1,0:T(8,128)}, u32[]{:S(2)}) copy-start(f32[8,1024]{1,0:T(8,128)} %get-tuple-element.57) | copy-start | bytes 98308
  220.2 14.8 %copy-start.1 = (f32[128,128]{0,1:T(8,128)S(1)}, f32[128,128]{0,1:T(8,128)}, u32[]{:S(2)}) copy-start(f32[128,128]{0,1:T(8,128)} %get-tuple-element.124) | copy-start | bytes 196612
  220.2 15.0 %copy-start.2 = (bf16[5120,16]{0,1:T(8,128)(2,1)S(1)}, bf16[5120,16]{0,1:T(8,128)(2,1)}, u32[]{:S(2)}) copy-start(bf16[5120,16]{0,1:T(8,128)(2,1)} %param.17) | copy-start | bytes 491524
  220.2 15.4 %copy-start.3 = (bf16[5120,16]{0,1:T(8,128)(2,1)S(1)}, bf16[5120,16]{0,1:T(8,128)(2,1)}, u32[]{:S(2)}) copy-start(bf16[5120,16]{0,1:T(8,128)(2,1)} %param.16) | copy-start | bytes 491524
  220.2 267.9 %all-to-all-start = ((f32[64,1,128,130]{2,1,3,0:T(1,128)}), f32[64,1,128,130]{2,1,3,0:T(1,128)}, u32[]{:S(2)}, u32[]{:S(2)}) async-start(f32[64,1,128,130]{2,1,3,0:T(1,128)} %copy.67), calls=%async_computation | async-start | bytes 8519680 | tf_op jit(solution)/shard_map/all_to_all | solution.py:50
  235.0 252.5 %copy-start.5 = (f32[128]{0:T(128)S(1)}, f32[128]{0:T(128)}, u32[]{:S(2)}) copy-start(f32[128]{0:T(128)} %param.19) | copy-start | bytes 1540
Sparse Core Ops, SparseCore 0:
  19.3 66.0 all-gather.5
  87.5 29.8 all-gather.7
where the time goes:
time: 502 us; the launch traced here: 500 us
  blocking collectives  256 us (51%)
  waiting for transfers between devices  98 us (20%)
  local copies, waits for them, and re-layouts  48.9 us (10%)
  matrix products  27.3 us (5%)
  loops' own time  22.5 us (4%)
  other arithmetic  17.5 us (3%)
  starting transfers between devices  14.8 us (3%)
  between operations  14.3 us (3%)
    all_gather x1, blocking collectives, gather_turned(): filled = lax.all_gather(both, axis, axis=0, tiled=True)  251 us
    all_gather x2, waiting for transfers between devices, gather_in_order(): pieces = lax.all_gather(pieces, axes[k])  98 us
    another operation x1, loops' own time, per_device(): lax.map(shard_term, jnp.arange(kv_heads, dtype=jnp.int32))  22.5 us
    dot_general x8, matrix products, shard_term(): jnp.dot(weights.astype(jnp.bfloat16), value_rows, preferred_element_type=...  15.3 us
    all_to_all x1, starting transfers between devices, sent_together(): lax.all_to_all(both, axis, split_axis=split_dim, concat_axis=concat_dim,...  14.7 us
    concatenate x1, local copies, waits for them, and re-layouts, sent_together(): both = jnp.concatenate(columns, axis=along)  12.4 us
    another operation x2, local copies, waits for them, and re-layouts, sent_together(): columns = [a.reshape(*a.shape[:along], -1) for a in arrays]  12.1 us
    dynamic_update_slice x16, local copies, waits for them, and re-layouts, per_device(): lax.map(shard_term, jnp.arange(kv_heads, dtype=jnp.int32))  11.7 us
  transfers between devices with their start and end apart: 3, of which 2 were waited for; matrix products, arithmetic and copies ran while one was open for 0% of the time, Pallas kernels for 0%

commit v1 on v0

--- a/solution.py
+++ b/solution.py
@@ -13,7 +13,9 @@
     turned = [jnp.moveaxis(a, dim, 0) for a, dim in zip(arrays, dims)]
     widths = [t[0].size for t in turned]
     both = jnp.concatenate([t.reshape(-1, w) for t, w in zip(turned, widths)], axis=1)
-    filled = lax.all_gather(both, axis, axis=0, tiled=True)
+    filled = jnp.concatenate(
+        lax.all_to_all(jnp.stack([both] * lax.axis_size(axis)), axis, 0, 0), axis=0
+    )
     pieces = jnp.split(filled, [sum(widths[:k]) for k in range(1, len(widths))], axis=1)
     return tuple(
         (

time: 502 us -> 442 us (0.88)
  blocking collectives: 256 us -> 5.71 us
  waiting for transfers between devices: 98 us -> 259 us
  starting transfers between devices: 14.8 us -> 36.8 us
    all_gather x1 -> x0, blocking collectives: 251 us -> none  [gather_turned(): filled = lax.all_gather(both, axis, axis=0, tiled=True)]
    all_to_all x1, waiting for transfers between devices: 0.01 us -> 185 us  [sent_together(): lax.all_to_all(both, axis, split_axis=split_dim, concat_axis=concat_dim,...]
    all_gather x2, waiting for transfers between devices: 98 us -> 74.2 us  [gather_in_order(): pieces = lax.all_gather(pieces, axes[k])]
    all_to_all x0 -> x1, starting transfers between devices: none -> 22 us  [gather_turned(): lax.all_to_all(jnp.stack([both] * lax.axis_size(axis)), axis, 0, 0)]
  transfers between devices with their start and end apart: 3 -> 4, of which waited for: 2 -> 3; matrix products, arithmetic and copies ran while one was open for 0% -> 20% of each run, Pallas kernels for 0% -> 0%
where the time goes in v1:
time: 442 us; the launch traced here: 435 us
  waiting for transfers between devices  259 us (59%)
  local copies, waits for them, and re-layouts  50.4 us (11%)
  starting transfers between devices  36.8 us (8%)
  matrix products  27.2 us (6%)
  loops' own time  22.5 us (5%)
  other arithmetic  19.3 us (4%)
  between operations  14.3 us (3%)
  blocking collectives  5.71 us (1%)
    all_to_all x1, waiting for transfers between devices, sent_together(): lax.all_to_all(both, axis, split_axis=split_dim, concat_axis=concat_dim,...  185 us
    all_gather x2, waiting for transfers between devices, gather_in_order(): pieces = lax.all_gather(pieces, axes[k])  74.2 us
    another operation x1, loops' own time, per_device(): lax.map(shard_term, jnp.arange(kv_heads, dtype=jnp.int32))  22.5 us
    all_to_all x1, starting transfers between devices, gather_turned(): lax.all_to_all(jnp.stack([both] * lax.axis_size(axis)), axis, 0, 0)  22 us
    dot_general x8, matrix products, shard_term(): jnp.dot(weights.astype(jnp.bfloat16), value_rows, preferred_element_type=...  15.4 us
    all_to_all x1, starting transfers between devices, sent_together(): lax.all_to_all(both, axis, split_axis=split_dim, concat_axis=concat_dim,...  14.7 us
    concatenate x1, local copies, waits for them, and re-layouts, sent_together(): both = jnp.concatenate(columns, axis=along)  12.4 us
    another operation x2, local copies, waits for them, and re-layouts, sent_together(): columns = [a.reshape(*a.shape[:along], -1) for a in arrays]  12.1 us
  transfers between devices with their start and end apart: 4, of which 3 were waited for; matrix products, arithmetic and copies ran while one was open for 20% of the time, Pallas kernels for 0%

profile of v1, /device:TPU:1, one launch (start us, length us, event | category | flops | bytes accessed | tf_op | source)
XLA Modules:
  0.0 435.2 jit_solution(3566522910754847145)
XLA Ops:
  6.6 1.3 copy-done
  7.9 2.0 multiply_reduce_fusion
  9.8 0.7 fusion.29
  11.4 1.3 pad_maximum_fusion.1
  12.7 5.7 %all-gather = bf16[256,128]{0,1:T(8,128)(2,1)S(1)} all-gather(bf16[128,128]{0,1:T(8,128)(2,1)S(1)} %get-tuple-element.123), channel_id=2, replica_groups=mesh['ctx_0'=16,'ctx_1'=2,'ctx_2'=2,'req'=8] {'ctx_1'}, dimensions={0}, use_global_device_ids=true | all-gather | bytes 98304 | tf_op jit(solution)/shard_map/all_gather | solution.py:37
  18.4 0.7 copy.60
  19.2 66.1 %all-gather.6.cloned.1.call-done = bf16[32,1,128,128]{3,2,1,0:T(8,128)(2,1)} async-done(((bf16[2,1,128,128]{3,2,1,0:T(8,128)(2,1)}), bf16[32,1,128,128]{3,2,1,0:T(8,128)(2,1)}) %all-gather.6.cloned.1.call-update) | async-done | bytes 1048592 | tf_op jit(solution)/shard_map/all_gather | solution.py:37
  86.3 0.9 stack.2
  87.2 22.0 %all-to-all-start = ((bf16[64,16,256]{2,1,0:T(8,128)(2,1)}), bf16[64,16,256]{2,1,0:T(8,128)(2,1)}, u32[]{:S(2)}, u32[]{:S(2)}) async-start(bf16[64,16,256]{2,1,0:T(8,128)(2,1)} %stack.2), calls=%async_computation | async-start | bytes 1048576 | tf_op jit(solution)/shard_map/all_to_all | solution.py:17
  109.3 8.0 %all-gather.8.cloned.1.call-done = bf16[32,2,1,128,128]{4,3,2,1,0:T(8,128)(2,1)} async-done(((bf16[16,2,1,128,128]{4,3,2,1,0:T(8,128)(2,1)}), bf16[32,2,1,128,128]{4,3,2,1,0:T(8,128)(2,1)}) %all-gather.8.cloned.1.call-update) | async-done | bytes 2097168 | tf_op jit(solution)/shard_map/all_gather | solution.py:37
  117.3 1.7 copy.54
  119.1 69.1 %while.16 = (s32[]{:T(128)}, f32[8,1024,128]{2,1,0:T(8,128)}, f32[8,1024]{1,0:T(8,128)S(1)}, f32[8,1024]{1,0:T(8,128)}, s32[8]{0:T(128)S(1)}, /*index=5*/bf16[8,...) while((s32[]{:T(128)}, f32[8,1024,128]{2,1,0:T(8,128)}, ...), condition=%wide.region_6.8_spmd.clone, body=%wide.region_3.7_spmd.clone.sunk | while | flops 68286728 | bytes 2459269 | solution.py:163
  119.1 0.7 dynamic_slice.37
  122.5 0.7 compare_bitcast_fusion.2
  123.2 1.0 fusion.68
  124.2 1.9 fusion.69
  126.2 1.4 dynamic_update_slice.20
  127.7 0.7 dynamic_slice.37
  131.2 0.7 compare_bitcast_fusion.2
  131.8 1.0 fusion.68
  132.8 2.0 fusion.69
  134.9 1.4 dynamic_update_slice.20
  136.4 0.7 dynamic_slice.37
  139.9 0.7 compare_bitcast_fusion.2
  140.5 1.0 fusion.68
  141.5 1.9 fusion.69
  143.5 1.4 dynamic_update_slice.20
  145.0 0.7 dynamic_slice.37
  148.5 0.7 compare_bitcast_fusion.2
  149.1 1.0 fusion.68
  150.1 1.9 fusion.69
  152.2 1.4 dynamic_update_slice.20
  153.6 0.7 dynamic_slice.37
  157.1 0.7 compare_bitcast_fusion.2
  157.7 1.0 fusion.68
  158.8 1.9 fusion.69
  160.8 1.4 dynamic_update_slice.20
  162.3 0.7 dynamic_slice.37
  165.7 0.7 compare_bitcast_fusion.2
  166.4 1.0 fusion.68
  167.4 1.9 fusion.69
  169.4 1.4 dynamic_update_slice.20
  170.9 0.7 dynamic_slice.37
  174.4 0.7 compare_bitcast_fusion.2
  175.0 1.0 fusion.68
  176.1 1.9 fusion.69
  178.1 1.4 dynamic_update_slice.20
  179.6 0.7 dynamic_slice.37
  183.0 0.7 compare_bitcast_fusion.2
  183.7 1.0 fusion.68
  184.7 1.9 fusion.69
  186.7 1.4 dynamic_update_slice.20
  188.2 6.0 %reshape_broadcast_in_dim_reshape.8 = f32[64,1,128,1]{3,2,0,1:T(8,128)} reshape(f32[8,1024]{1,0:T(8,128)S(1)} %get-tuple-element.56) | data formatting | bytes 65536 | tf_op jit(solution)/shard_map/reshape;broadcast_in_dim;reshape | solution.py:49
  194.2 6.1 %reshape_broadcast_in_dim_reshape.9 = f32[64,1,128,1]{3,2,0,1:T(8,128)} reshape(f32[8,1024]{1,0:T(8,128)S(1)} %copy-done.4) | data formatting | bytes 65536 | tf_op jit(solution)/shard_map/reshape;broadcast_in_dim;reshape | solution.py:49
  200.3 7.6 %pad_maximum_fusion = f32[64,1,128,130]{3,2,0,1:T(8,128)} fusion(f32[64,1,128,1]{3,2,0,1:T(8,128)} %reshape_broadcast_in_dim_reshape.9, f32[64,1,128,1]{3,2,0,1:T(8,128)} %reshape_broadcast_in_dim_reshape.8, f32[64,1,128,128]{3,2,0,1:T(8,128)} %bitcast.104), kind=kLoop, calls=%fused_computation.19 | loop fusion | flops 2129920 | bytes 8519680 | tf_op jit(solution)/shard_map/concatenate | solution.py:50
  207.9 12.4 %copy.57 = f32[64,1,128,130]{2,1,3,0:T(1,128)} copy(f32[64,1,128,130]{3,2,0,1:T(8,128)} %pad_maximum_fusion) | data formatting | bytes 8519680 | tf_op jit(solution)/shard_map/concatenate | solution.py:50
  220.3 14.7 %all-to-all-start.1 = ((f32[64,1,128,130]{2,1,3,0:T(1,128)}), f32[64,1,128,130]{2,1,3,0:T(1,128)}, u32[]{:S(2)}, u32[]{:S(2)}) async-start(f32[64,1,128,130]{2,1,3,0:T(1,128)} %copy.57), calls=%async_computation.1 | async-start | bytes 8519680 | tf_op jit(solution)/shard_map/all_to_all | solution.py:52
  235.0 1.1 fusion.22
  236.1 1.1 fusion.24
  237.6 1.0 slice_bitcast_fusion
  239.0 184.8 %all-to-all-done.1 = f32[64,1,128,130]{2,1,3,0:T(1,128)} async-done(((f32[64,1,128,130]{2,1,3,0:T(1,128)}), f32[64,1,128,130]{2,1,3,0:T(1,128)}, u32[]{:S(2)}, u32[]{:S(2)}) %all-to-all-start.1) | async-done | bytes 4259872 | tf_op jit(solution)/shard_map/all_to_all | solution.py:52
  423.8 2.8 copy.62
  426.7 0.7 fusion.17
  427.6 0.8 fusion.21
  (56 shorter events, 3.6 us)
Async XLA Ops:
  6.5 1.3 copy-start
  6.5 78.9 %copy-start.2 = (bf16[5120,16]{0,1:T(8,128)(2,1)S(1)}, bf16[5120,16]{0,1:T(8,128)(2,1)}, u32[]{:S(2)}) copy-start(bf16[5120,16]{0,1:T(8,128)(2,1)} %param.17) | copy-start | bytes 491524
  6.5 79.3 %copy-start.3 = (bf16[5120,16]{0,1:T(8,128)(2,1)S(1)}, bf16[5120,16]{0,1:T(8,128)(2,1)}, u32[]{:S(2)}) copy-start(bf16[5120,16]{0,1:T(8,128)(2,1)} %param.16) | copy-start | bytes 491524
  6.5 78.8 %all-gather.6.cloned.1.call-start = ((), (), s32[]{:S(2)}) async-start(), calls=%async_computation.2 | async-start | bytes 1114112 | tf_op jit(solution)/shard_map/all_gather | solution.py:37
  19.2 98.1 %all-gather.8.cloned.1.call-start = ((), (), s32[]{:S(2)}) async-start(), calls=%async_computation.3 | async-start | bytes 3145728 | tf_op jit(solution)/shard_map/all_gather | solution.py:37
  87.2 133.1 %all-to-all-start = ((bf16[64,16,256]{2,1,0:T(8,128)(2,1)}), bf16[64,16,256]{2,1,0:T(8,128)(2,1)}, u32[]{:S(2)}, u32[]{:S(2)}) async-start(bf16[64,16,256]{2,1,0:T(8,128)(2,1)} %stack.2), calls=%async_computation | async-start | bytes 1048576 | tf_op jit(solution)/shard_map/all_to_all | solution.py:17
  188.2 6.1 %copy-start.4 = (f32[8,1024]{1,0:T(8,128)S(1)}, f32[8,1024]{1,0:T(8,128)}, u32[]{:S(2)}) copy-start(f32[8,1024]{1,0:T(8,128)} %get-tuple-element.57) | copy-start | bytes 98308
  220.2 15.9 %copy-start.5 = (f32[128]{0:T(128)S(1)}, f32[128]{0:T(128)}, u32[]{:S(2)}) copy-start(f32[128]{0:T(128)} %param.19) | copy-start | bytes 1540
  220.2 17.1 %copy-start.1 = (f32[128,128]{0,1:T(8,128)S(1)}, f32[128,128]{0,1:T(8,128)}, u32[]{:S(2)}) copy-start(f32[128,128]{0,1:T(8,128)} %get-tuple-element.124) | copy-start | bytes 196612
  220.3 203.6 %all-to-all-start.1 = ((f32[64,1,128,130]{2,1,3,0:T(1,128)}), f32[64,1,128,130]{2,1,3,0:T(1,128)}, u32[]{:S(2)}, u32[]{:S(2)}) async-start(f32[64,1,128,130]{2,1,3,0:T(1,128)} %copy.57), calls=%async_computation.1 | async-start | bytes 8519680 | tf_op jit(solution)/shard_map/all_to_all | solution.py:52
Sparse Core Ops, SparseCore 0:
  19.3 66.0 all-gather.5
  87.5 29.8 all-gather.7
